TPU v7x, 8 devices: a whole 2x2x1 slice. The times are simulated.
8 devices in a mesh: vp: 8 (over z, y, x, core).
Axes of the slice: x: 2, y: 2, z: 1, core: 2. Of those that a mesh axis runs over, the one named last changes fastest.
Arguments:
- hidden: bfloat16 [128, 1536], replicated
- ln_weight: bfloat16 [1536], replicated
- ln_bias: bfloat16 [1536], replicated
- embedding: bfloat16 [250880, 1536], P('vp')
- temperature: float32 [], replicated
- cand_ids: int32 [128, 128], replicated
Outputs:
- output 1: float32 [128, 250880], P(None, 'vp')
- output 2: float32 [128, 128], replicated
All inputs are finite; a program needn't handle non-finite values.
Results may differ from a plain program's by a relative error of at most 0.001.
Values sent between devices are 32-bit elements.
A program may use at most 1 GiB of HBM per device.

v0:
```python
import jax
import jax.numpy as jnp
from jax import lax
from jax.sharding import PartitionSpec as P, NamedSharding


def layer_norm(hidden, ln_weight, ln_bias):
    hidden_f32 = hidden.astype(jnp.float32)
    row_mean = jnp.mean(hidden_f32, axis=-1, keepdims=True)
    centered = hidden_f32 - row_mean
    row_var = jnp.mean(centered * centered, axis=-1, keepdims=True)
    scaled = centered * lax.rsqrt(row_var + 1e-5)
    return (scaled * ln_weight.astype(jnp.float32) + ln_bias.astype(jnp.float32)).astype(jnp.bfloat16)


def solution(mesh):
    axis_name = mesh.axis_names[0]

    def per_device(hidden, ln_weight, ln_bias, emb_shard, value_a11, cand_ids):
        normed = layer_norm(hidden, ln_weight, ln_bias)
        shard_logits = lax.dot_general(normed, emb_shard, (((1,), (1,)), ((), ())), preferred_element_type=jnp.float32) / value_a11
        full_logits = lax.all_gather(shard_logits, axis_name, axis=1, tiled=True)
        row_max = jnp.max(full_logits, axis=1, keepdims=True)
        exp_sum = jnp.sum(jnp.exp(full_logits - row_max), axis=1, keepdims=True)
        log_norm = row_max + jnp.log(exp_sum)
        shard_lp = shard_logits - log_norm
        cand_lp = jnp.take_along_axis(full_logits, cand_ids, axis=1) - log_norm
        return shard_lp, cand_lp

    return jax.shard_map(
        per_device,
        mesh=mesh,
        in_specs=(P(), P(), P(), P(axis_name, None), P(), P()),
        out_specs=(P(None, axis_name), P()),
        check_vma=False,
    )
```

profile of v0, /device:TPU:0, one launch (start us, length us, event | category | flops | bytes accessed | tf_op | source)
XLA Modules:
  0.0 914.1 jit_solution(11089166095649408889)
XLA Ops:
  7.2 0.0 all-gather.2.cloned.1.call-start
  7.9 1.1 convert_reduce_fusion
  9.0 1.2 fusion.2
  10.3 0.7 convert_element_type.13
  10.9 0.7 convert_element_type.14
  11.6 42.5 %convolution_divide_fusion = f32[128,31360]{1,0:T(8,128)} fusion(bf16[31360,1536]{1,0:T(8,128)(2,1)} %param.9, f32[]{:T(128)S(6)} %copy.8, bf16[128,1536]{1,0:T(8,128)(2,1)} %param.6, f32[1536]{0:T(1024)S(1)} %convert_element_type.14, f32[1536]{0:T(1024)S(1)} %convert_element_type.13, f32[128]{0:T(128)S(1)} %add_rsqrt_fusion, f32[128]{0:T(128)S(1)} %broadcast_multiply_fusion), kind=kOutput, calls=%fused_computation.2 | convolution fusion | flops 12336447488 | bytes 112800768 | tf_op jit(solution)/shard_map/dot_general | solution.py:21
  54.2 0.0 copy-start
  54.2 0.0 all-gather.2.cloned.1.call-update
  54.2 0.8 copy-done
  55.0 559.0 %all-gather.2.cloned.1.call-done = f32[128,250880]{1,0:T(8,128)} async-done(((f32[128,31360]{1,0:T(8,128)}), f32[128,250880]{1,0:T(8,128)}) %all-gather.2.cloned.1.call-update) | async-done | bytes 128450576 | tf_op jit(solution)/shard_map/all_gather | solution.py:22
  614.0 38.8 %reduce_max.9 = f32[128]{0:T(128)S(1)} reduce(f32[128,250880]{1,0:T(8,128)} %all-gather.2.cloned.1.call-done, f32[]{:T(128)} %constant.21.clone.1), dimensions={1}, to_apply=%region_2.0 | reduce | flops 32112512 | bytes 128451072 | tf_op jit(solution)/shard_map/reduce_max | solution.py:23
  652.8 39.3 %exponential_reduce_fusion = f32[128]{0:T(128)S(1)} fusion(f32[128,250880]{1,0:T(8,128)} %all-gather.2.cloned.1.call-done, f32[128]{0:T(128)S(1)} %reduce_max.9), kind=kLoop, calls=%fused_computation.1 | loop fusion | flops 64225152 | bytes 128451584 | tf_op jit(solution)/shard_map/reduce_sum | solution.py:24
  692.1 11.3 %broadcast_subtract_fusion = f32[128,31360]{1,0:T(8,128)} fusion(f32[128,31360]{1,0:T(8,128)} %convolution_divide_fusion, f32[128]{0:T(128)S(1)} %log_add_fusion), kind=kLoop, calls=%fused_computation.3 | loop fusion | flops 4014080 | bytes 32113152 | tf_op jit(solution)/shard_map/sub | solution.py:26
  703.4 203.2 %gather_fusion = f32[16384]{0:T(1024)S(1)} fusion(f32[128,250880]{1,0:T(8,128)} %all-gather.2.cloned.1.call-done, s32[16384]{0:T(1024)S(1)} %fusion.12), kind=kCustom, calls=%fused_computation | custom fusion | bytes 262144 | tf_op jit(solution)/shard_map/jit(take_along_axis)/gather | solution.py:27
  906.6 0.7 fusion.11
  (4 shorter events, 0.0 us)
Async XLA Ops:
  7.2 606.8 %all-gather.2.cloned.1.call-start = ((), (), s32[]{:S(2)}) async-start(), calls=%async_computation | async-start | bytes 144506880 | tf_op jit(solution)/shard_map/all_gather | solution.py:22
  54.2 0.8 copy-start
Sparse Core Ops, SparseCore 0:
  54.3 559.6 all-gather.1
where the time goes:
time: 921 us; the launch traced here: 914 us
  waiting for transfers between devices  559 us (61%)
  local copies, waits for them, and re-layouts  204 us (22%)
  other arithmetic  93.9 us (10%)
  matrix products  42.5 us (5%)
  between operations  14.7 us (2%)
    all_gather x1, waiting for transfers between devices, per_device(): full_logits = lax.all_gather(shard_logits, axis_name, axis=1, tiled=True)  559 us
    gather x1, local copies, waits for them, and re-layouts, per_device(): cand_lp = jnp.take_along_axis(full_logits, cand_ids, axis=1) - log_norm  203 us
    dot_general x1, matrix products, per_device(): lax.dot_general(normed, emb_shard, (((1,), (1,)), ((), ())), preferred_el...  42.5 us
    reduce_sum x1, other arithmetic, per_device(): exp_sum = jnp.sum(jnp.exp(full_logits - row_max), axis=1, keepdims=True)  39.3 us
    reduce_max x1, other arithmetic, per_device(): row_max = jnp.max(full_logits, axis=1, keepdims=True)  38.8 us
  transfers between devices with their start and end apart: 1, of which 1 were waited for; matrix products, arithmetic and copies ran while one was open for 0% of the time, Pallas kernels for 0%

commit v1 on v0

v1 whole, which is shorter than its diff:
```python
import functools

import jax
import jax.numpy as jnp
from jax import lax
from jax.experimental import pallas as pl
from jax.experimental.pallas import tpu as pltpu
from jax.sharding import PartitionSpec as P

MESH_ID = pl.DeviceIdType.MESH
LANES = 128
TILE = 1792
DEPTH = 4


def split_columns(columns, tile):
    full = columns // tile
    return full, columns - full * tile


def head_kernel(
    axis_name, n_dev, tile, full, rest,
    temp_ref, x_ref, w_ref, b_ref, cand_ref, emb_ref,
    z_ref, logz_ref, q_ref,
    ebuf, raw_a, raw_b, normed, m_ref, l_ref, cand_hi, cand_lo, q_part,
    stat_send, stat_recv, qrs_recv, q_own, q_all,
    e_sem, stat_ssem, stat_rsem, rs_ssem, rs_rsem, ag_ssem, ag_rsem,
):
    me = lax.axis_index(axis_name)
    rows, _ = x_ref.shape
    columns = emb_ref.shape[0]
    depth = ebuf.shape[0]
    groups = rows // 8
    own_rows = rows // n_dev

    def load(t, slot):
        return pltpu.make_async_copy(
            emb_ref.at[pl.ds(pl.multiple_of(t * tile, LANES), tile)], ebuf.at[slot], e_sem.at[slot])

    def load_rest(slot):
        return pltpu.make_async_copy(
            emb_ref.at[pl.ds(full * tile, rest)], ebuf.at[slot, pl.ds(0, rest)], e_sem.at[slot])

    def start_any(t):
        if t < full:
            load(t, t % depth).start()
        elif t == full and rest:
            load_rest(t % depth).start()

    barrier = pltpu.get_barrier_semaphore()
    for k in range(1, n_dev):
        pl.semaphore_signal(barrier, inc=1, device_id=(lax.rem(me + k, n_dev),), device_id_type=MESH_ID)
    for t in range(depth - 1):
        start_any(t)

    xf = x_ref[...].astype(jnp.float32)
    mean = jnp.mean(xf, axis=-1, keepdims=True)
    cent = xf - mean
    var = jnp.mean(cent * cent, axis=-1, keepdims=True)
    scaled = cent * lax.rsqrt(var + 1e-5)
    normed[...] = (scaled * w_ref[...].astype(jnp.float32) + b_ref[...].astype(jnp.float32)).astype(jnp.bfloat16)
    local = cand_ref[...] - me * columns
    cand_hi[...] = local >> 7
    cand_lo[...] = local & (LANES - 1)
    m_ref[...] = jnp.full_like(m_ref, -jnp.inf)
    l_ref[...] = jnp.zeros_like(l_ref)
    q_part[...] = jnp.zeros_like(q_part)
    inv_t = 1.0 / jnp.full((8, LANES), temp_ref[0, 0], jnp.float32)

    def dot(slot, raw, width):
        raw[:, :width] = lax.dot_general(
            normed[...], ebuf[slot, :width], (((1,), (1,)), ((), ())), preferred_element_type=jnp.float32)

    def epilogue(t, raw, width):
        for g in range(groups):
            r = pl.ds(8 * g, 8)
            zs = []
            for j in range(width // LANES):
                z = raw[r, j * LANES:(j + 1) * LANES] * inv_t
                z_ref[r, pl.ds(pl.multiple_of(t * tile + j * LANES, LANES), LANES)] = z
                zs.append(z)
            top = functools.reduce(jnp.maximum, zs)
            m_old = m_ref[r, :]
            m_new = jnp.maximum(m_old, top)
            total = l_ref[r, :] * jnp.exp(m_old - m_new)
            hi, lo = cand_hi[r, :], cand_lo[r, :]
            q = q_part[r, :]
            for j, z in enumerate(zs):
                total = total + jnp.exp(z - m_new)
                picked = jnp.take_along_axis(z, lo, axis=1, mode="promise_in_bounds")
                q = jnp.where(hi == t * (tile // LANES) + j, picked, q)
            m_ref[r, :] = m_new
            l_ref[r, :] = total
            q_part[r, :] = q

    raws = (raw_a, raw_b)

    load(0, 0).wait()
    start_any(depth - 1)
    dot(0, raw_a, tile)

    def step(t, parity):
        slot = lax.rem(t, depth)
        load(t, slot).wait()
        nxt = t + depth - 1

        @pl.when(nxt < full)
        def _():
            load(nxt, lax.rem(nxt, depth)).start()

        if rest:
            @pl.when(nxt == full)
            def _():
                load_rest(full % depth).start()

        dot(slot, raws[parity], tile)
        epilogue(t - 1, raws[1 - parity], tile)

    pairs = (full - 1) // 2

    def pair(i, carry):
        step(1 + 2 * i, 1)
        step(2 + 2 * i, 0)
        return carry

    lax.fori_loop(0, pairs, pair, 0)
    last = 2 * pairs
    if last < full - 1:
        last += 1
        step(jnp.int32(last), 1)
    if rest:
        load_rest(full % depth).wait()
        dot(full % depth, raws[(last + 1) % 2], rest)
        epilogue(last, raws[last % 2], tile)
        epilogue(full, raws[(last + 1) % 2], rest)
    else:
        epilogue(last, raws[last % 2], tile)

    m_t = m_ref[...].T
    top = jnp.max(m_t, axis=0, keepdims=True)
    total = jnp.sum(l_ref[...].T * jnp.exp(m_t - top), axis=0, keepdims=True)
    sub = lax.broadcasted_iota(jnp.int32, (8, LANES), 0)
    stats = jnp.where(sub == 0, jnp.broadcast_to(top, (8, LANES)), jnp.broadcast_to(total, (8, LANES)))
    stat_send[...] = stats
    stat_recv[me] = stats

    pl.semaphore_wait(barrier, n_dev - 1)

    def stat_copy(k):
        peer = lax.rem(me + k, n_dev)
        return pltpu.make_async_remote_copy(
            src_ref=stat_send, dst_ref=stat_recv.at[me], send_sem=stat_ssem.at[k], recv_sem=stat_rsem.at[k],
            device_id=(peer,), device_id_type=MESH_ID)

    def rs_copy(k):
        peer = lax.rem(me + k, n_dev)
        return pltpu.make_async_remote_copy(
            src_ref=q_part.at[pl.ds(pl.multiple_of(peer * own_rows, 8), own_rows)], dst_ref=qrs_recv.at[k],
            send_sem=rs_ssem.at[k], recv_sem=rs_rsem.at[k], device_id=(peer,), device_id_type=MESH_ID)

    def ag_copy(k):
        peer = lax.rem(me + k, n_dev)
        return pltpu.make_async_remote_copy(
            src_ref=q_own, dst_ref=q_all.at[pl.ds(pl.multiple_of(me * own_rows, 8), own_rows)],
            send_sem=ag_ssem.at[k], recv_sem=ag_rsem.at[k], device_id=(peer,), device_id_type=MESH_ID)

    stat_copies = [stat_copy(k) for k in range(1, n_dev)]
    rs_copies = [rs_copy(k) for k in range(1, n_dev)]
    ag_copies = [ag_copy(k) for k in range(1, n_dev)]
    for c in stat_copies:
        c.start()
    for c in rs_copies:
        c.start()
    for c in rs_copies:
        c.wait()
    mine = pl.ds(pl.multiple_of(me * own_rows, 8), own_rows)
    own = q_part[mine, :]
    for k in range(1, n_dev):
        own = own + qrs_recv[k]
    q_own[...] = own
    for c in ag_copies:
        c.start()
    for c in stat_copies:
        c.wait()
    every = stat_recv[...]
    tops = every[:, 0, :]
    sums = every[:, 1, :]
    top = jnp.max(tops, axis=0, keepdims=True)
    total = jnp.sum(sums * jnp.exp(tops - top), axis=0, keepdims=True)
    logz = top + jnp.log(total)
    logz_ref[...] = jnp.broadcast_to(logz, (LANES, rows)).T
    for c in ag_copies:
        c.wait()
    q_all[mine, :] = own
    q_ref[...] = q_all[...]


def write_kernel(z_ref, logz_ref, q_ref, lp_ref, cand_lp_ref, stage, sem):
    rows, columns = z_ref.shape
    groups = rows // 8
    depth = stage.shape[0]

    def put(g):
        return pltpu.make_async_copy(stage.at[g % depth], lp_ref.at[pl.ds(8 * g, 8)], sem.at[g % depth])

    for g in range(groups):
        if g >= depth:
            put(g - depth).wait()
        r = pl.ds(8 * g, 8)
        norm = logz_ref[r, :]
        for j in range(columns // LANES):
            c = slice(j * LANES, (j + 1) * LANES)
            stage[g % depth, :, c] = z_ref[r, c] - norm
        put(g).start()
    cand_lp_ref[...] = q_ref[...] - logz_ref[...]
    for g in range(groups - depth, groups):
        put(g).wait()


def solution(mesh):
    axis_name = mesh.axis_names[0]
    n_dev = mesh.shape[axis_name]

    def per_device(hidden, ln_weight, ln_bias, emb_shard, temperature, cand_ids):
        rows, feat = hidden.shape
        columns = emb_shard.shape[0]
        cands = cand_ids.shape[1]
        full, rest = split_columns(columns, TILE)
        f32 = jnp.float32
        vmem = pl.BlockSpec(memory_space=pltpu.VMEM)
        own_rows = rows // n_dev
        z, logz, q = pl.pallas_call(
            functools.partial(head_kernel, axis_name, n_dev, TILE, full, rest),
            out_shape=(
                pltpu.VMEM((rows, columns), f32),
                pltpu.VMEM((rows, LANES), f32),
                pltpu.VMEM((rows, cands), f32),
            ),
            in_specs=[pl.BlockSpec(memory_space=pltpu.SMEM)] + [vmem] * 4 + [pl.BlockSpec(memory_space=pl.ANY)],
            out_specs=(vmem, vmem, vmem),
            scratch_shapes=[
                pltpu.VMEM((DEPTH, TILE, feat), jnp.bfloat16),
                pltpu.VMEM((rows, TILE), f32),
                pltpu.VMEM((rows, TILE), f32),
                pltpu.VMEM((rows, feat), jnp.bfloat16),
                pltpu.VMEM((rows, LANES), f32),
                pltpu.VMEM((rows, LANES), f32),
                pltpu.VMEM((rows, cands), jnp.int32),
                pltpu.VMEM((rows, cands), jnp.int32),
                pltpu.VMEM((rows, cands), f32),
                pltpu.VMEM((8, LANES), f32),
                pltpu.VMEM((n_dev, 8, LANES), f32),
                pltpu.VMEM((n_dev, own_rows, cands), f32),
                pltpu.VMEM((own_rows, cands), f32),
                pltpu.VMEM((rows, cands), f32),
                pltpu.SemaphoreType.DMA((DEPTH,)),
                pltpu.SemaphoreType.DMA((n_dev,)),
                pltpu.SemaphoreType.DMA((n_dev,)),
                pltpu.SemaphoreType.DMA((n_dev,)),
                pltpu.SemaphoreType.DMA((n_dev,)),
                pltpu.SemaphoreType.DMA((n_dev,)),
                pltpu.SemaphoreType.DMA((n_dev,)),
            ],
            compiler_params=pltpu.CompilerParams(
                collective_id=0, has_side_effects=True, vmem_limit_bytes=44 * 1024 * 1024),
            name="head",
        )(temperature.reshape(1, 1), hidden, ln_weight.reshape(1, feat), ln_bias.reshape(1, feat), cand_ids, emb_shard)
        lp = z - logz[:, :1]
        cand_lp = q - logz
        return lp, cand_lp

    return jax.shard_map(
        per_device,
        mesh=mesh,
        in_specs=(P(), P(), P(), P(axis_name, None), P(), P()),
        out_specs=(P(None, axis_name), P()),
        check_vma=False,
    )
```

time: 921 us -> 60.1 us (0.07)
  waiting for transfers between devices: 559 us -> 0 us
  local copies, waits for them, and re-layouts: 204 us -> 2.67 us
  other arithmetic: 93.9 us -> 6.77 us
  Pallas kernels: 0 us -> 49.2 us
  matrix products: 42.5 us -> 0 us
  between operations: 14.7 us -> 1.29 us
    all_gather x1 -> x0, waiting for transfers between devices: 559 us -> none  [per_device(): full_logits = lax.all_gather(shard_logits, axis_name, axis=1, tiled=True)]
    gather x1 -> x0, local copies, waits for them, and re-layouts: 203 us -> none  [per_device(): cand_lp = jnp.take_along_axis(full_logits, cand_ids, axis=1) - log_norm]
    pallas_call x0 -> x1, Pallas kernels: none -> 49.2 us  [per_device(): pl.pallas_call(functools.partial(head_kernel, axis_name, n_dev, TILE, ful...]
    dot_general x1 -> x0, matrix products: 42.5 us -> none  [per_device(): lax.dot_general(normed, emb_shard, (((1,), (1,)), ((), ())), preferred_el...]
    reduce_sum x3 -> x0, other arithmetic: 41.7 us -> none  [the longest x1 39.3 us: per_device(): exp_sum = jnp.sum(jnp.exp(full_logits - row_max), axis=1, keepdims=True)]
    reduce_max x1 -> x0, other arithmetic: 38.8 us -> none  [per_device(): row_max = jnp.max(full_logits, axis=1, keepdims=True)]
  transfers between devices with their start and end apart: 1 -> 0, of which waited for: 1 -> 0; matrix products, arithmetic and copies ran while one was open for 0% -> 0% of each run, Pallas kernels for 0% -> 0%
where the time goes in v1:
time: 60.1 us; the launch traced here: 59.9 us
  Pallas kernels  49.2 us (82%)
  other arithmetic  6.77 us (11%)
  local copies, waits for them, and re-layouts  2.67 us (4%)
  between operations  1.29 us (2%)
    pallas_call x1, Pallas kernels, per_device(): pl.pallas_call(functools.partial(head_kernel, axis_name, n_dev, TILE, ful...  49.2 us
    sub x1, other arithmetic, per_device(): lp = z - logz[:, :1]  6.12 us
    reshape x1, local copies, waits for them, and re-layouts, per_device(): ln_weight.reshape(1, feat)  1.29 us
    reshape x1, local copies, waits for them, and re-layouts, per_device(): ln_bias.reshape(1, feat)  1.28 us

profile of v1, /device:TPU:0, one launch (start us, length us, event | category | flops | bytes accessed | tf_op | source)
XLA Modules:
  0.0 59.9 jit_solution(2481039778016706396)
XLA Ops:
  1.3 1.3 %reshape.14.w_ref = bf16[1,1536]{1,0:T(2,128)(2,1)} reshape(bf16[1536]{0:T(1024)(128)(2,1)} %param.7) | data formatting | bytes 6144 | tf_op jit(solution)/shard_map/reshape | solution.py:267
  2.6 1.3 %reshape.15.b_ref = bf16[1,1536]{1,0:T(2,128)(2,1)} reshape(bf16[1536]{0:T(1024)(128)(2,1)} %param.8) | data formatting | bytes 6144 | tf_op jit(solution)/shard_map/reshape | solution.py:267
  3.8 49.2 %head.1 = (f32[128,31360]{1,0:T(8,128)S(1)}, f32[128,128]{1,0:T(8,128)S(1)}, f32[128,128]{1,0:T(8,128)S(1)}) custom-call(f32[1,1]{1,0:T(1,128)} %bitcast.1.temp_ref, bf16[128,1536]{1,0:T(8,128)(2,1)} %x_ref.1, bf16[1,1536]{1,0:T(2,128)(2,1)} %reshape.14.w_ref, bf16[1,1536]{1,0:T(2,128)(2,1)} %reshape.15.b_ref, s32[128,128]{1,0:T(8,128)} %cand_ref.1, ...), custom_call_target="tpu_custom_call" | custom-call | tf_op jit(solution)/shard_map/head/pallas_call | solution.py:232
  53.0 0.1 slice_reduce_fusion
  53.1 0.6 %sub.16 = f32[128,128]{1,0:T(8,128)} subtract(f32[128,128]{1,0:T(8,128)S(1)} %get-tuple-element.7, f32[128,128]{1,0:T(8,128)S(1)} %get-tuple-element.6) | non-fusion elementwise | flops 16384 | bytes 196608 | tf_op jit(solution)/shard_map/sub | solution.py:269
  53.8 6.1 %broadcast_subtract_fusion = f32[128,31360]{1,0:T(8,128)} fusion(f32[128,31360]{1,0:T(8,128)S(1)} %get-tuple-element.5, f32[128]{0:T(128)S(1)} %slice_reduce_fusion), kind=kLoop, calls=%fused_computation | loop fusion | flops 4014080 | bytes 32113152 | tf_op jit(solution)/shard_map/sub | solution.py:268

commit v2 on v0

v2 whole, which is shorter than its diff:
```python
import functools

import jax
import jax.numpy as jnp
from jax import lax
from jax.experimental import pallas as pl
from jax.experimental.pallas import tpu as pltpu
from jax.sharding import PartitionSpec as P

MESH_ID = pl.DeviceIdType.MESH
LANES = 128
MXU = 256
TILE = 640
UNROLL = 7
DEPTH = 14
ACC_OF = (0, 1, 0, 1, 0, 1, 2)


def head_kernel(
    axis_name,
    temp_ref, x_ref, w_ref, b_ref, cand_ref, emb_ref,
    z_ref, stat_ref, q_ref,
    ebuf, raw, zbuf, normed, m_ref, l_ref, cand_hi, cand_lo, e_sem,
):
    me = lax.axis_index(axis_name)
    rows, feat = x_ref.shape
    columns = emb_ref.shape[0]
    tiles = columns // TILE
    passes = feat // MXU
    half = TILE // 2
    blocks = TILE // LANES

    def load(t, slot):
        return pltpu.make_async_copy(
            emb_ref.at[pl.ds(pl.multiple_of(t * TILE, LANES), TILE)], ebuf.at[slot], e_sem.at[slot])

    for t in range(DEPTH - 1):
        load(t, t).start()

    xf = x_ref[...].astype(jnp.float32)
    mean = jnp.mean(xf, axis=-1, keepdims=True)
    cent = xf - mean
    var = jnp.mean(cent * cent, axis=-1, keepdims=True)
    scaled = cent * lax.rsqrt(var + 1e-5)
    normed[:rows, :] = (
        scaled * w_ref[...].astype(jnp.float32)[None] + b_ref[...].astype(jnp.float32)[None]).astype(jnp.bfloat16)
    normed[rows:, :] = jnp.zeros((MXU - rows, feat), jnp.bfloat16)
    local = cand_ref[...] - me * columns
    cand_hi[...] = local >> 7
    cand_lo[...] = local & (LANES - 1)
    m_ref[...] = jnp.full_like(m_ref, -jnp.inf)
    l_ref[...] = jnp.zeros_like(l_ref)
    q_ref[...] = jnp.zeros_like(q_ref)
    raw[UNROLL - 1] = jnp.zeros_like(raw[UNROLL - 1])
    inv_t = 1.0 / jnp.full((8, LANES), temp_ref[0, 0], jnp.float32)

    def push(k):
        for q in range(2):
            pltpu.matmul_push_rhs(
                normed[:, k * MXU:(k + 1) * MXU], staging_register=k % 2, mxu_index=q, transpose=True)

    def epilogue(t, i, first):
        column = jnp.maximum(t, 0) * TILE
        base = jnp.where(first, -(1 << 26), t * blocks)
        for j in range(blocks):
            c = slice(j * LANES, (j + 1) * LANES)
            zbuf[i % 2, :, c] = raw[i, c, :].T
        for g in range(rows // 8):
            r = pl.ds(8 * g, 8)
            zs = []
            for j in range(blocks):
                z = zbuf[i % 2, r, j * LANES:(j + 1) * LANES] * inv_t
                z_ref[r, pl.ds(pl.multiple_of(column + j * LANES, LANES), LANES)] = z
                zs.append(z)
            m_old = m_ref[r, :]
            m_new = jnp.maximum(m_old, functools.reduce(jnp.maximum, zs))
            total = l_ref[r, :] * jnp.exp(m_old - m_new)
            hi, lo = cand_hi[r, :], cand_lo[r, :]
            q = q_ref[r, :]
            for j, z in enumerate(zs):
                total = total + jnp.exp(z - m_new)
                picked = jnp.take_along_axis(z, lo, axis=1, mode="promise_in_bounds")
                q = jnp.where(hi == base + j, picked, q)
            if first is not False:
                m_new = jnp.where(first, -jnp.inf, m_new)
                total = jnp.where(first, 0.0, total)
            m_ref[r, :] = m_new
            l_ref[r, :] = total
            q_ref[r, :] = q

    def body(*accs):
        accs = (accs[:3], accs[3:])

        def pop(i):
            for q in range(2):
                raw[i, q * half:(q + 1) * half, :] = pltpu.matmul_pop(accs[q][ACC_OF[i]])[:, :LANES]

        def trip(it, carry):
            for i in range(UNROLL):
                t = it * UNROLL + i
                slot = lax.rem(t, DEPTH)
                load(t, slot).wait()
                nxt = t + DEPTH - 1

                @pl.when(nxt < tiles)
                def _():
                    load(nxt, lax.rem(nxt, DEPTH)).start()

                for k in range(passes):
                    for q in range(2):
                        pltpu.matmul_acc_lhs(
                            accs[q][ACC_OF[i]],
                            ebuf[slot, q * half:(q + 1) * half, k * MXU:(k + 1) * MXU],
                            load_staged_rhs=k % 2)
                    push((k + 1) % passes)
                    if k == 1 and i > 0:
                        pop(i - 1)
                if i == 0:
                    epilogue(t - 1, UNROLL - 1, it == 0)
                else:
                    epilogue(t - 1, i - 1, False)
            pop(UNROLL - 1)
            return carry

        push(0)
        lax.fori_loop(0, tiles // UNROLL, trip, 0)
        for q in range(2):
            pltpu.matmul_acc_lhs(accs[q][2], jnp.zeros((half, MXU), jnp.bfloat16), load_staged_rhs=0)
        epilogue(jnp.int32(tiles - 1), UNROLL - 1, False)
        for q in range(2):
            raw[0, q * half:(q + 1) * half, :] = pltpu.matmul_pop(accs[q][2])[:, :LANES]

    shape = ((half, MXU), jnp.float32)
    pl.run_scoped(body, *[pltpu.ACC(0)(*shape)] * 3, *[pltpu.ACC(1)(*shape)] * 3)

    m_t = m_ref[...].T
    top = jnp.max(m_t, axis=0, keepdims=True)
    total = jnp.sum(l_ref[...].T * jnp.exp(m_t - top), axis=0, keepdims=True)
    sub = lax.broadcasted_iota(jnp.int32, (8, LANES), 0)
    stat_ref[...] = jnp.where(sub == 0, jnp.broadcast_to(top, (8, LANES)), jnp.broadcast_to(total, (8, LANES)))


def exchange_kernel(
    axis_name, n_dev,
    stat_ref, part_ref, logz_ref, q_ref,
    stat_recv, rs_recv, q_own, q_all,
    stat_ssem, stat_rsem, rs_ssem, rs_rsem, ag_ssem, ag_rsem,
):
    me = lax.axis_index(axis_name)
    rows = part_ref.shape[0]
    own_rows = rows // n_dev
    barrier = pltpu.get_barrier_semaphore()
    for k in range(1, n_dev):
        pl.semaphore_signal(barrier, inc=1, device_id=(lax.rem(me + k, n_dev),), device_id_type=MESH_ID)
    pl.semaphore_wait(barrier, n_dev - 1)

    def stat_copy(k):
        peer = lax.rem(me + k, n_dev)
        return pltpu.make_async_remote_copy(
            src_ref=stat_ref, dst_ref=stat_recv.at[k], send_sem=stat_ssem.at[k], recv_sem=stat_rsem.at[k],
            device_id=(peer,), device_id_type=MESH_ID)

    def rs_copy(k):
        peer = lax.rem(me + k, n_dev)
        return pltpu.make_async_remote_copy(
            src_ref=part_ref.at[pl.ds(pl.multiple_of(peer * own_rows, 8), own_rows)], dst_ref=rs_recv.at[k],
            send_sem=rs_ssem.at[k], recv_sem=rs_rsem.at[k], device_id=(peer,), device_id_type=MESH_ID)

    def ag_copy(k):
        peer = lax.rem(me + k, n_dev)
        return pltpu.make_async_remote_copy(
            src_ref=q_own, dst_ref=q_all.at[pl.ds(pl.multiple_of(me * own_rows, 8), own_rows)],
            send_sem=ag_ssem.at[k], recv_sem=ag_rsem.at[k], device_id=(peer,), device_id_type=MESH_ID)

    stat_copies = [stat_copy(k) for k in range(1, n_dev)]
    rs_copies = [rs_copy(k) for k in range(1, n_dev)]
    ag_copies = [ag_copy(k) for k in range(1, n_dev)]
    for c in rs_copies + stat_copies:
        c.start()
    stat_recv[0] = stat_ref[...]
    mine = pl.ds(pl.multiple_of(me * own_rows, 8), own_rows)
    own = part_ref[mine, :]
    for c in rs_copies:
        c.wait()
    for k in range(1, n_dev):
        own = own + rs_recv[k]
    q_own[...] = own
    for c in ag_copies:
        c.start()
    for c in stat_copies:
        c.wait()
    tops = stat_recv[:, 0, :]
    sums = stat_recv[:, 1, :]
    top = jnp.max(tops, axis=0, keepdims=True)
    total = jnp.sum(sums * jnp.exp(tops - top), axis=0, keepdims=True)
    logz = jnp.broadcast_to(top + jnp.log(total), (LANES, rows)).T
    logz_ref[...] = logz
    for c in ag_copies:
        c.wait()
    q_all[mine, :] = own
    q_ref[...] = q_all[...] - logz


def solution(mesh):
    axis_name = mesh.axis_names[0]
    n_dev = mesh.shape[axis_name]

    def per_device(hidden, ln_weight, ln_bias, emb_shard, temperature, cand_ids):
        rows, feat = hidden.shape
        columns = emb_shard.shape[0]
        cands = cand_ids.shape[1]
        own_rows = rows // n_dev
        f32 = jnp.float32
        vmem = pl.BlockSpec(memory_space=pltpu.VMEM)
        z, stat, part = pl.pallas_call(
            functools.partial(head_kernel, axis_name),
            out_shape=(
                pltpu.VMEM((rows, columns), f32),
                pltpu.VMEM((8, LANES), f32),
                pltpu.VMEM((rows, cands), f32),
            ),
            in_specs=[pl.BlockSpec(memory_space=pltpu.SMEM)] + [vmem] * 4 + [pl.BlockSpec(memory_space=pl.ANY)],
            out_specs=(vmem, vmem, vmem),
            scratch_shapes=[
                pltpu.VMEM((DEPTH, TILE, feat), jnp.bfloat16),
                pltpu.VMEM((UNROLL, TILE, rows), f32),
                pltpu.VMEM((2, rows, TILE), f32),
                pltpu.VMEM((MXU, feat), jnp.bfloat16),
                pltpu.VMEM((rows, LANES), f32),
                pltpu.VMEM((rows, LANES), f32),
                pltpu.VMEM((rows, cands), jnp.int32),
                pltpu.VMEM((rows, cands), jnp.int32),
                pltpu.SemaphoreType.DMA((DEPTH,)),
            ],
            compiler_params=pltpu.CompilerParams(vmem_limit_bytes=44 * 1024 * 1024),
            name="head",
        )(temperature.reshape(1, 1), hidden, ln_weight, ln_bias, cand_ids, emb_shard)
        logz, cand_lp = pl.pallas_call(
            functools.partial(exchange_kernel, axis_name, n_dev),
            out_shape=(
                pltpu.VMEM((rows, LANES), f32),
                pltpu.VMEM((rows, cands), f32),
            ),
            in_specs=[vmem, vmem],
            out_specs=(vmem, vmem),
            scratch_shapes=[
                pltpu.VMEM((n_dev, 8, LANES), f32),
                pltpu.VMEM((n_dev, own_rows, cands), f32),
                pltpu.VMEM((own_rows, cands), f32),
                pltpu.VMEM((rows, cands), f32),
            ] + [pltpu.SemaphoreType.DMA((n_dev,))] * 6,
            compiler_params=pltpu.CompilerParams(
                collective_id=0, has_side_effects=True, vmem_limit_bytes=4 * 1024 * 1024),
            name="exchange",
        )(stat, part)
        return z - logz[:, :1], cand_lp

    return jax.shard_map(
        per_device,
        mesh=mesh,
        in_specs=(P(), P(), P(), P(axis_name, None), P(), P()),
        out_specs=(P(None, axis_name), P()),
        check_vma=False,
    )
```

time: 921 us -> 50.4 us (0.05)
  waiting for transfers between devices: 559 us -> 0 us
  local copies, waits for them, and re-layouts: 204 us -> 0.73 us
  other arithmetic: 93.9 us -> 6.15 us
  matrix products: 42.5 us -> 0 us
  Pallas kernels: 0 us -> 42.1 us
  between operations: 14.7 us -> 1.3 us
    all_gather x1 -> x0, waiting for transfers between devices: 559 us -> none  [per_device(): full_logits = lax.all_gather(shard_logits, axis_name, axis=1, tiled=True)]
    gather x1 -> x0, local copies, waits for them, and re-layouts: 203 us -> none  [per_device(): cand_lp = jnp.take_along_axis(full_logits, cand_ids, axis=1) - log_norm]
    dot_general x1 -> x0, matrix products: 42.5 us -> none  [per_device(): lax.dot_general(normed, emb_shard, (((1,), (1,)), ((), ())), preferred_el...]
    pallas_call x0 -> x2, Pallas kernels: none -> 42.1 us  [the longest x1 31 us: per_device(): pl.pallas_call(functools.partial(head_kernel, axis_name), out_shape=(pltp...]
    reduce_sum x3 -> x0, other arithmetic: 41.7 us -> none  [the longest x1 39.3 us: per_device(): exp_sum = jnp.sum(jnp.exp(full_logits - row_max), axis=1, keepdims=True)]
    reduce_max x1 -> x0, other arithmetic: 38.8 us -> none  [per_device(): row_max = jnp.max(full_logits, axis=1, keepdims=True)]
  transfers between devices with their start and end apart: 1 -> 0, of which waited for: 1 -> 0; matrix products, arithmetic and copies ran while one was open for 0% -> 0% of each run, Pallas kernels for 0% -> 0%
where the time goes in v2:
time: 50.4 us; the launch traced here: 50.3 us
  Pallas kernels  42.1 us (84%)
  other arithmetic  6.15 us (12%)
  between operations  1.3 us (3%)
  local copies, waits for them, and re-layouts  0.73 us (1%)
    pallas_call x1, Pallas kernels, per_device(): pl.pallas_call(functools.partial(head_kernel, axis_name), out_shape=(pltp...  31 us
    pallas_call x1, Pallas kernels, per_device(): pl.pallas_call(functools.partial(exchange_kernel, axis_name, n_dev), out_...  11.1 us
    sub x1, other arithmetic, per_device(): return (z - logz[:, :1], cand_lp)  6.15 us

profile of v2, /device:TPU:0, one launch (start us, length us, event | category | flops | bytes accessed | tf_op | source)
XLA Modules:
  0.0 50.3 jit_solution(5190019174346458065)
XLA Ops:
  1.3 31.0 %head.1 = (f32[128,31360]{1,0:T(8,128)S(1)}, f32[8,128]{1,0:T(8,128)S(1)}, f32[128,128]{1,0:T(8,128)S(1)}) custom-call(f32[1,1]{1,0:T(1,128)} %bitcast.1.temp_ref, bf16[128,1536]{1,0:T(8,128)(2,1)} %x_ref.1, bf16[1536]{0:T(1024)(128)(2,1)} %w_ref.1, bf16[1536]{0:T(1024)(128)(2,1)} %b_ref.1, s32[128,128]{1,0:T(8,128)} %cand_ref.1, bf16[31360,1536]{1,0:T(8,128)(2,1)} %emb_ref.1), custom_call_target="tpu_custom_call" | custom-call | tf_op jit(solution)/shard_map/head/pallas_call | solution.py:215
  32.3 11.1 %exchange.1 = (f32[128,128]{1,0:T(8,128)S(1)}, f32[128,128]{1,0:T(8,128)S(1)}) custom-call(f32[8,128]{1,0:T(8,128)S(1)} %get-tuple-element.8.stat_ref, f32[128,128]{1,0:T(8,128)S(1)} %get-tuple-element.9.part_ref), custom_call_target="tpu_custom_call" | custom-call | tf_op jit(solution)/shard_map/exchange/pallas_call | solution.py:238
  43.4 0.1 slice_reduce_fusion
  43.5 6.1 %broadcast_subtract_fusion = f32[128,31360]{1,0:T(8,128)} fusion(f32[128,31360]{1,0:T(8,128)S(1)} %get-tuple-element.7, f32[128]{0:T(128)S(1)} %slice_reduce_fusion), kind=kLoop, calls=%fused_computation | loop fusion | flops 4014080 | bytes 32113152 | tf_op jit(solution)/shard_map/sub | solution.py:256
  49.7 0.6 %copy.9 = f32[128,128]{1,0:T(8,128)} copy(f32[128,128]{1,0:T(8,128)S(1)} %get-tuple-element.13) | data formatting | bytes 131072

commit v3 on v2

--- a/solution.py
+++ b/solution.py
@@ -12,18 +12,18 @@
 MXU = 256
 TILE = 640
 UNROLL = 7
-DEPTH = 14
+DEPTH = 6
 ACC_OF = (0, 1, 0, 1, 0, 1, 2)
 
 
 def head_kernel(
     axis_name,
-    temp_ref, x_ref, w_ref, b_ref, cand_ref, emb_ref,
+    temp_ref, x_hbm, w_hbm, b_hbm, cand_hbm, emb_ref,
     z_ref, stat_ref, q_ref,
-    ebuf, raw, zbuf, normed, m_ref, l_ref, cand_hi, cand_lo, e_sem,
+    ebuf, raw, zbuf, normed, m_ref, l_ref, cand_hi, cand_lo, x_ref, w_ref, b_ref, cand_ref, e_sem, s_sem,
 ):
     me = lax.axis_index(axis_name)
-    rows, feat = x_ref.shape
+    rows, feat = x_hbm.shape
     columns = emb_ref.shape[0]
     tiles = columns // TILE
     passes = feat // MXU
@@ -34,7 +34,16 @@
         return pltpu.make_async_copy(
             emb_ref.at[pl.ds(pl.multiple_of(t * TILE, LANES), TILE)], ebuf.at[slot], e_sem.at[slot])
 
-    for t in range(DEPTH - 1):
+    small = [
+        pltpu.make_async_copy(src, dst, s_sem.at[i])
+        for i, (src, dst) in enumerate(((x_hbm, x_ref), (w_hbm, w_ref), (b_hbm, b_ref), (cand_hbm, cand_ref)))]
+    for c in small:
+        c.start()
+    for t in range(2):
+        load(t, t).start()
+    for c in small:
+        c.wait()
+    for t in range(2, DEPTH - 1):
         load(t, t).start()
 
     xf = x_ref[...].astype(jnp.float32)
@@ -201,6 +210,17 @@
     q_ref[...] = q_all[...] - logz
 
 
+def write_kernel(z_ref, logz_ref, q_ref, lp_ref, cand_lp_ref):
+    columns = z_ref.shape[1]
+    for g in range(4):
+        r = slice(8 * g, 8 * g + 8)
+        norm = logz_ref[r, :]
+        for j in range(columns // LANES):
+            c = slice(j * LANES, (j + 1) * LANES)
+            lp_ref[r, c] = z_ref[r, c] - norm
+    cand_lp_ref[...] = q_ref[...]
+
+
 def solution(mesh):
     axis_name = mesh.axis_names[0]
     n_dev = mesh.shape[axis_name]
@@ -219,7 +239,7 @@
                 pltpu.VMEM((8, LANES), f32),
                 pltpu.VMEM((rows, cands), f32),
             ),
-            in_specs=[pl.BlockSpec(memory_space=pltpu.SMEM)] + [vmem] * 4 + [pl.BlockSpec(memory_space=pl.ANY)],
+            in_specs=[pl.BlockSpec(memory_space=pltpu.SMEM)] + [pl.BlockSpec(memory_space=pl.ANY)] * 5,
             out_specs=(vmem, vmem, vmem),
             scratch_shapes=[
                 pltpu.VMEM((DEPTH, TILE, feat), jnp.bfloat16),
@@ -230,7 +250,12 @@
                 pltpu.VMEM((rows, LANES), f32),
                 pltpu.VMEM((rows, cands), jnp.int32),
                 pltpu.VMEM((rows, cands), jnp.int32),
+                pltpu.VMEM((rows, feat), jnp.bfloat16),
+                pltpu.VMEM((feat,), jnp.bfloat16),
+                pltpu.VMEM((feat,), jnp.bfloat16),
+                pltpu.VMEM((rows, cands), jnp.int32),
                 pltpu.SemaphoreType.DMA((DEPTH,)),
+                pltpu.SemaphoreType.DMA((4,)),
             ],
             compiler_params=pltpu.CompilerParams(vmem_limit_bytes=44 * 1024 * 1024),
             name="head",
@@ -253,7 +278,19 @@
                 collective_id=0, has_side_effects=True, vmem_limit_bytes=4 * 1024 * 1024),
             name="exchange",
         )(stat, part)
-        return z - logz[:, :1], cand_lp
+        lp, cand_out = pl.pallas_call(
+            write_kernel,
+            grid=(rows // 32,),
+            out_shape=(
+                jax.ShapeDtypeStruct((rows, columns), f32),
+                jax.ShapeDtypeStruct((rows, cands), f32),
+            ),
+            in_specs=[pl.BlockSpec((32, columns), lambda i: (i, 0)), pl.BlockSpec((32, LANES), lambda i: (i, 0)), pl.BlockSpec((32, cands), lambda i: (i, 0))],
+            out_specs=(pl.BlockSpec((32, columns), lambda i: (i, 0)), pl.BlockSpec((32, cands), lambda i: (i, 0))),
+            compiler_params=pltpu.CompilerParams(vmem_limit_bytes=24 * 1024 * 1024),
+            name="write",
+        )(z, logz, cand_lp)
+        return lp, cand_out
 
     return jax.shard_map(
         per_device,

time: 50.4 us -> 49 us (0.972)
  other arithmetic: 6.15 us -> 0 us
  Pallas kernels: 42.1 us -> 47.6 us
  local copies, waits for them, and re-layouts: 0.73 us -> 0 us
    sub x1 -> x0, other arithmetic: 6.15 us -> none  [per_device(): return (z - logz[:, :1], cand_lp)]
    pallas_call x0 -> x1, Pallas kernels: none -> 6.11 us  [per_device(): pl.pallas_call(write_kernel, grid=(rows // 32,), out_shape=(jax.ShapeDtyp...]
    unnamed x1 -> x0, local copies, waits for them, and re-layouts: 0.63 us -> none
    pallas_call x1, Pallas kernels: 31 us -> 30.4 us  [per_device(): pl.pallas_call(functools.partial(head_kernel, axis_name), out_shape=(pltp...]
where the time goes in v3:
time: 49 us; the launch traced here: 48.9 us
  Pallas kernels  47.6 us (97%)
  between operations  1.29 us (3%)
    pallas_call x1, Pallas kernels, per_device(): pl.pallas_call(functools.partial(head_kernel, axis_name), out_shape=(pltp...  30.4 us
    pallas_call x1, Pallas kernels, per_device(): pl.pallas_call(functools.partial(exchange_kernel, axis_name, n_dev), out_...  11.1 us
    pallas_call x1, Pallas kernels, per_device(): pl.pallas_call(write_kernel, grid=(rows // 32,), out_shape=(jax.ShapeDtyp...  6.11 us

profile of v3, /device:TPU:0, one launch (start us, length us, event | category | flops | bytes accessed | tf_op | source)
XLA Modules:
  0.0 48.9 jit_solution(6890814161738697350)
XLA Ops:
  1.3 30.4 %head.1 = (f32[128,31360]{1,0:T(8,128)S(1)}, f32[8,128]{1,0:T(8,128)S(1)}, f32[128,128]{1,0:T(8,128)S(1)}) custom-call(f32[1,1]{1,0:T(1,128)} %bitcast.1.temp_ref, bf16[128,1536]{1,0:T(8,128)(2,1)} %x_hbm.1, bf16[1536]{0:T(1024)(128)(2,1)} %w_hbm.1, bf16[1536]{0:T(1024)(128)(2,1)} %b_hbm.1, s32[128,128]{1,0:T(8,128)} %cand_hbm.1, bf16[31360,1536]{1,0:T(8,128)(2,1)} %emb_ref.1), custom_call_target="tpu_custom_call" | custom-call | tf_op jit(solution)/shard_map/head/pallas_call | solution.py:235
  31.7 11.1 %exchange.1 = (f32[128,128]{1,0:T(8,128)S(1)}, f32[128,128]{1,0:T(8,128)S(1)}) custom-call(f32[8,128]{1,0:T(8,128)S(1)} %get-tuple-element.8.stat_ref, f32[128,128]{1,0:T(8,128)S(1)} %get-tuple-element.9.part_ref), custom_call_target="tpu_custom_call" | custom-call | tf_op jit(solution)/shard_map/exchange/pallas_call | solution.py:263
  42.8 6.1 %write.1 = (f32[128,31360]{1,0:T(8,128)}, f32[128,128]{1,0:T(8,128)}) custom-call(f32[128,31360]{1,0:T(8,128)S(1)} %get-tuple-element.7.z_ref, f32[128,128]{1,0:T(8,128)S(1)} %get-tuple-element.10.logz_ref, f32[128,128]{1,0:T(8,128)S(1)} %get-tuple-element.11.q_ref), custom_call_target="tpu_custom_call" | custom-call | tf_op jit(solution)/shard_map/write/pallas_call | solution.py:281

commit v4 on v3

v4 whole, which is shorter than its diff:
```python
import functools

import jax
import jax.numpy as jnp
from jax import lax
from jax.experimental import pallas as pl
from jax.experimental.pallas import tpu as pltpu
from jax.sharding import PartitionSpec as P

MESH_ID = pl.DeviceIdType.MESH
LANES = 128
MXU = 256
TILE = 640
UNROLL = 6
DEPTH = 8
ACCS = 3


def head_kernel(
    axis_name,
    temp_ref, x_hbm, w_hbm, b_hbm, cand_hbm, emb_ref,
    z_ref, e_tail, normed, m_ref, l_ref, q_ref, cand_hi, cand_lo, inv_ref,
    ebuf, raw, zbuf, x_ref, w_ref, b_ref, cand_ref, e_sem, s_sem, tail_sem,
):
    me = lax.axis_index(axis_name)
    rows, feat = x_hbm.shape
    columns = emb_ref.shape[0]
    tiles = columns // TILE - 1
    passes = feat // MXU
    half = TILE // 2
    blocks = TILE // LANES

    def load(t, slot):
        return pltpu.make_async_copy(
            emb_ref.at[pl.ds(pl.multiple_of(t * TILE, LANES), TILE)], ebuf.at[slot], e_sem.at[slot])

    tail = pltpu.make_async_copy(emb_ref.at[pl.ds(tiles * TILE, TILE)], e_tail, tail_sem)
    small = [
        pltpu.make_async_copy(src, dst, s_sem.at[i])
        for i, (src, dst) in enumerate(((x_hbm, x_ref), (w_hbm, w_ref), (b_hbm, b_ref), (cand_hbm, cand_ref)))]
    for c in small:
        c.start()
    for t in range(2):
        load(t, t).start()
    for c in small:
        c.wait()
    for t in range(2, DEPTH - 1):
        load(t, t).start()

    xf = x_ref[...].astype(jnp.float32)
    mean = jnp.mean(xf, axis=-1, keepdims=True)
    cent = xf - mean
    var = jnp.mean(cent * cent, axis=-1, keepdims=True)
    scaled = cent * lax.rsqrt(var + 1e-5)
    normed[:rows, :] = (
        scaled * w_ref[...].astype(jnp.float32)[None] + b_ref[...].astype(jnp.float32)[None]).astype(jnp.bfloat16)
    normed[rows:, :] = jnp.zeros((MXU - rows, feat), jnp.bfloat16)
    local = cand_ref[...] - me * columns
    cand_hi[...] = local >> 7
    cand_lo[...] = local & (LANES - 1)
    m_ref[...] = jnp.full_like(m_ref, -jnp.inf)
    l_ref[...] = jnp.zeros_like(l_ref)
    q_ref[...] = jnp.zeros_like(q_ref)
    raw[UNROLL - 1] = jnp.zeros_like(raw[UNROLL - 1])
    inv_t = 1.0 / jnp.full((8, LANES), temp_ref[0, 0], jnp.float32)
    inv_ref[...] = inv_t

    def push(k):
        for q in range(2):
            pltpu.matmul_push_rhs(
                normed[:, k * MXU:(k + 1) * MXU], staging_register=k % 2, mxu_index=q, transpose=True)

    def epilogue(t, i, first):
        column = jnp.maximum(t, 0) * TILE
        base = jnp.where(first, -(1 << 26), t * blocks)
        for j in range(blocks):
            c = slice(j * LANES, (j + 1) * LANES)
            zbuf[i % 2, :, c] = raw[i, c, :].T
        for g in range(rows // 8):
            r = pl.ds(8 * g, 8)
            zs = []
            for j in range(blocks):
                z = zbuf[i % 2, r, j * LANES:(j + 1) * LANES] * inv_t
                z_ref[r, pl.ds(pl.multiple_of(column + j * LANES, LANES), LANES)] = z
                zs.append(z)
            m_old = m_ref[r, :]
            m_new = jnp.maximum(m_old, functools.reduce(jnp.maximum, zs))
            total = l_ref[r, :] * jnp.exp(m_old - m_new)
            hi, lo = cand_hi[r, :], cand_lo[r, :]
            q = q_ref[r, :]
            for j, z in enumerate(zs):
                total = total + jnp.exp(z - m_new)
                picked = jnp.take_along_axis(z, lo, axis=1, mode="promise_in_bounds")
                q = jnp.where(hi == base + j, picked, q)
            if first is not False:
                m_new = jnp.where(first, -jnp.inf, m_new)
                total = jnp.where(first, 0.0, total)
            m_ref[r, :] = m_new
            l_ref[r, :] = total
            q_ref[r, :] = q

    def body(*accs):
        accs = (accs[:ACCS], accs[ACCS:])

        def pop(i):
            for q in range(2):
                raw[i, q * half:(q + 1) * half, :] = pltpu.matmul_pop(accs[q][i % ACCS])[:, :LANES]

        def trip(it, carry):
            for i in range(UNROLL):
                t = it * UNROLL + i
                slot = lax.rem(t, DEPTH)
                load(t, slot).wait()
                nxt = t + DEPTH - 1

                @pl.when(nxt < tiles)
                def _():
                    load(nxt, lax.rem(nxt, DEPTH)).start()

                @pl.when(nxt == tiles)
                def _():
                    tail.start()

                for k in range(passes):
                    for q in range(2):
                        pltpu.matmul_acc_lhs(
                            accs[q][i % ACCS],
                            ebuf[slot, q * half:(q + 1) * half, k * MXU:(k + 1) * MXU],
                            load_staged_rhs=k % 2)
                    push((k + 1) % passes)
                    if k == 1:
                        pop((i - 1) % UNROLL)
                epilogue(t - 1, (i - 1) % UNROLL, it == 0 if i == 0 else False)
            return carry

        for i in range(ACCS):
            pop(i)
        push(0)
        lax.fori_loop(0, tiles // UNROLL, trip, 0)
        pop(UNROLL - 1)
        for q in range(2):
            pltpu.matmul_acc_lhs(accs[q][0], jnp.zeros((half, MXU), jnp.bfloat16), load_staged_rhs=0)
        epilogue(jnp.int32(tiles - 1), UNROLL - 1, False)
        pop(0)

    shape = ((half, MXU), jnp.float32)
    pl.run_scoped(body, *[pltpu.ACC(0)(*shape)] * ACCS, *[pltpu.ACC(1)(*shape)] * ACCS)
    tail.wait()


def flipped(me, mask):
    peer = me
    for bit in (1, 2, 4):
        if mask & bit:
            peer = peer + bit * (1 - 2 * lax.rem(me // bit, 2))
    return peer


def exchange_kernel(
    axis_name, n_dev, last_block,
    e_ref, normed, m_in, l_in, q_in, cand_hi, cand_lo, inv_ref,
    z_ref, logz_ref, q_ref,
    raw, zbuf, m_ref, l_ref, send, recv, q_own, q_all, stat_send, stat_recv,
    rs_sem, stat_sem, ag_sem,
):
    me = lax.axis_index(axis_name)
    rows = m_in.shape[0]
    own_rows = rows // n_dev
    blocks = TILE // LANES
    barrier = pltpu.get_barrier_semaphore()
    order = sorted(range(1, n_dev), key=lambda k: (-(k // 2).bit_count(), k))
    peers = {k: flipped(me, k) for k in order}
    for k in order:
        pl.semaphore_signal(barrier, inc=1, device_id=(peers[k],), device_id_type=MESH_ID)
    for h in range(2):
        rr = slice(h * (TILE // 2), (h + 1) * (TILE // 2))
        raw[rr, :] = lax.dot_general(
            e_ref[rr, :], normed[:rows, :], (((1,), (1,)), ((), ())), preferred_element_type=jnp.float32)
    for j in range(blocks):
        c = slice(j * LANES, (j + 1) * LANES)
        zbuf[:, c] = raw[c, :].T
    inv_t = inv_ref[...]
    for g in range(rows // 8):
        r = pl.ds(8 * g, 8)
        zs = []
        for j in range(blocks):
            c = slice(j * LANES, (j + 1) * LANES)
            z = zbuf[r, c] * inv_t
            z_ref[r, c] = z
            zs.append(z)
        m_old = m_in[r, :]
        m_new = jnp.maximum(m_old, functools.reduce(jnp.maximum, zs))
        total = l_in[r, :] * jnp.exp(m_old - m_new)
        hi, lo = cand_hi[r, :], cand_lo[r, :]
        q = q_in[r, :]
        for j, z in enumerate(zs):
            total = total + jnp.exp(z - m_new)
            picked = jnp.take_along_axis(z, lo, axis=1, mode="promise_in_bounds")
            q = jnp.where(hi == last_block + j, picked, q)
        m_ref[r, :] = m_new
        l_ref[r, :] = total
        per = own_rows // 8
        send[g // per, 8 * (g % per):8 * (g % per) + 8, :] = q
    m_t = m_ref[...].T
    top = jnp.max(m_t, axis=0, keepdims=True)
    total = jnp.sum(l_ref[...].T * jnp.exp(m_t - top), axis=0, keepdims=True)
    stat_send[0:1, :] = top
    stat_send[1:2, :] = total
    stat_recv[0] = stat_send[...]
    pl.semaphore_wait(barrier, n_dev - 1)

    def copy(k, src, dst, sems):
        return pltpu.make_async_remote_copy(
            src_ref=src, dst_ref=dst, send_sem=sems.at[0, k], recv_sem=sems.at[1, k],
            device_id=(peers[k],), device_id_type=MESH_ID)

    rs_copies = [copy(k, send.at[peers[k]], recv.at[k], rs_sem) for k in order]
    stat_copies = [copy(k, stat_send, stat_recv.at[k], stat_sem) for k in order]
    ag_copies = [copy(k, q_own, q_all.at[me], ag_sem) for k in order]
    for c in rs_copies + stat_copies:
        c.start()
    own = send[me]
    for c in reversed(rs_copies):
        c.wait_recv()
    for k in range(1, n_dev):
        own = own + recv[k]
    q_own[...] = own
    for c in ag_copies:
        c.start()
    q_all[me] = own
    for c in stat_copies:
        c.wait_recv()
    tops = stat_recv[:, 0, :]
    sums = stat_recv[:, 1, :]
    top = jnp.max(tops, axis=0, keepdims=True)
    total = jnp.sum(sums * jnp.exp(tops - top), axis=0, keepdims=True)
    logz = jnp.broadcast_to(top + jnp.log(total), (LANES, rows)).T
    logz_ref[...] = logz
    for c in rs_copies + stat_copies:
        c.wait_send()
    for c in reversed(ag_copies):
        c.wait_recv()
    for d in range(n_dev):
        r = slice(d * own_rows, (d + 1) * own_rows)
        q_ref[r, :] = q_all[d] - logz[r, :]
    for c in ag_copies:
        c.wait_send()


def write_kernel(z_ref, tail_ref, logz_ref, q_ref, lp_ref, cand_lp_ref):
    columns = z_ref.shape[1]
    for g in range(z_ref.shape[0] // 8):
        r = slice(8 * g, 8 * g + 8)
        norm = logz_ref[r, :]
        for j in range(columns // LANES):
            c = slice(j * LANES, (j + 1) * LANES)
            lp_ref[r, c] = z_ref[r, c] - norm
        for j in range(TILE // LANES):
            c = slice(j * LANES, (j + 1) * LANES)
            lp_ref[r, columns + j * LANES:columns + (j + 1) * LANES] = tail_ref[r, c] - norm
    cand_lp_ref[...] = q_ref[...]


def solution(mesh):
    axis_name = mesh.axis_names[0]
    n_dev = mesh.shape[axis_name]

    def per_device(hidden, ln_weight, ln_bias, emb_shard, temperature, cand_ids):
        rows, feat = hidden.shape
        columns = emb_shard.shape[0]
        cands = cand_ids.shape[1]
        own_rows = rows // n_dev
        f32 = jnp.float32
        vmem = pl.BlockSpec(memory_space=pltpu.VMEM)
        main = columns - TILE
        square, square_int = pltpu.VMEM((rows, LANES), f32), pltpu.VMEM((rows, cands), jnp.int32)
        z, *state = pl.pallas_call(
            functools.partial(head_kernel, axis_name),
            out_shape=(
                pltpu.VMEM((rows, main), f32), pltpu.VMEM((TILE, feat), jnp.bfloat16),
                pltpu.VMEM((MXU, feat), jnp.bfloat16), square, square, square, square_int, square_int,
                pltpu.VMEM((8, LANES), f32),
            ),
            in_specs=[pl.BlockSpec(memory_space=pltpu.SMEM)] + [pl.BlockSpec(memory_space=pl.ANY)] * 5,
            out_specs=(vmem,) * 9,
            scratch_shapes=[
                pltpu.VMEM((DEPTH, TILE, feat), jnp.bfloat16),
                pltpu.VMEM((UNROLL, TILE, rows), f32),
                pltpu.VMEM((2, rows, TILE), f32),
                pltpu.VMEM((rows, feat), jnp.bfloat16),
                pltpu.VMEM((feat,), jnp.bfloat16),
                pltpu.VMEM((feat,), jnp.bfloat16),
                pltpu.VMEM((rows, cands), jnp.int32),
                pltpu.SemaphoreType.DMA((DEPTH,)),
                pltpu.SemaphoreType.DMA((4,)),
                pltpu.SemaphoreType.DMA,
            ],
            compiler_params=pltpu.CompilerParams(vmem_limit_bytes=40 * 1024 * 1024),
            name="head",
        )(temperature.reshape(1, 1), hidden, ln_weight, ln_bias, cand_ids, emb_shard)
        z_tail, logz, q = pl.pallas_call(
            functools.partial(exchange_kernel, axis_name, n_dev, main // LANES),
            out_shape=(pltpu.VMEM((rows, TILE), f32), square, square),
            in_specs=[vmem] * 8,
            out_specs=(vmem,) * 3,
            scratch_shapes=[
                pltpu.VMEM((TILE, rows), f32),
                pltpu.VMEM((rows, TILE), f32),
                square, square,
                pltpu.VMEM((n_dev, own_rows, cands), f32),
                pltpu.VMEM((n_dev, own_rows, cands), f32),
                pltpu.VMEM((own_rows, cands), f32),
                pltpu.VMEM((n_dev, own_rows, cands), f32),
                pltpu.VMEM((2, LANES), f32),
                pltpu.VMEM((n_dev, 2, LANES), f32),
            ] + [pltpu.SemaphoreType.DMA((2, n_dev))] * 3,
            compiler_params=pltpu.CompilerParams(
                collective_id=0, has_side_effects=True, vmem_limit_bytes=8 * 1024 * 1024),
            name="exchange",
        )(*state)
        return pl.pallas_call(
            write_kernel,
            grid=(rows // 32,),
            out_shape=(
                jax.ShapeDtypeStruct((rows, columns), f32),
                jax.ShapeDtypeStruct((rows, cands), f32),
            ),
            in_specs=[pl.BlockSpec((32, n), lambda i: (i, 0)) for n in (main, TILE, LANES, cands)],
            out_specs=(pl.BlockSpec((32, columns), lambda i: (i, 0)), pl.BlockSpec((32, cands), lambda i: (i, 0))),
            compiler_params=pltpu.CompilerParams(vmem_limit_bytes=24 * 1024 * 1024),
            name="write",
        )(z, z_tail, logz, q)

    return jax.shard_map(
        per_device,
        mesh=mesh,
        in_specs=(P(), P(), P(), P(axis_name, None), P(), P()),
        out_specs=(P(None, axis_name), P()),
        check_vma=False,
    )
```

time: 49 us -> 48.2 us (0.984)
  Pallas kernels: 47.6 us -> 46.8 us
    pallas_call x1, Pallas kernels: 30.4 us -> 29.7 us  [per_device(): pl.pallas_call(functools.partial(head_kernel, axis_name), out_shape=(pltp...]
where the time goes in v4:
time: 48.2 us; the launch traced here: 48.1 us
  Pallas kernels  46.8 us (97%)
  between operations  1.29 us (3%)
    pallas_call x1, Pallas kernels, per_device(): pl.pallas_call(functools.partial(head_kernel, axis_name), out_shape=(pltp...  29.7 us
    pallas_call x1, Pallas kernels, per_device(): pl.pallas_call(functools.partial(exchange_kernel, axis_name, n_dev, main...  11 us
    pallas_call x1, Pallas kernels, per_device(): pl.pallas_call(write_kernel, grid=(rows // 32,), out_shape=(jax.ShapeDtyp...  6.11 us

profile of v4, /device:TPU:0, one launch (start us, length us, event | category | flops | bytes accessed | tf_op | source)
XLA Modules:
  0.0 48.1 jit_solution(13613965873529845298)
XLA Ops:
  1.3 29.7 %head.1 = (f32[128,30720]{1,0:T(8,128)S(1)}, bf16[640,1536]{1,0:T(8,128)(2,1)S(1)}, bf16[256,1536]{1,0:T(8,128)(2,1)S(1)}, f32[128,128]{1,0:T(8,128)S(1)}, f32[1...) custom-call(f32[1,1]{1,0:T(1,128)} %bitcast.1.temp_ref, ...), custom_call_target="tpu_custom_call" | custom-call | tf_op jit(solution)/shard_map/head/pallas_call | solution.py:277
  31.0 11.0 %exchange.1 = (f32[128,640]{1,0:T(8,128)S(1)}, f32[128,128]{1,0:T(8,128)S(1)}, f32[128,128]{1,0:T(8,128)S(1)}) custom-call(bf16[640,1536]{1,0:T(8,128)(2,1)S(1)} %get-tuple-element.15.e_ref, bf16[256,1536]{1,0:T(8,128)(2,1)S(1)} %get-tuple-element.16.normed, f32[128,128]{1,0:T(8,128)S(1)} %get-tuple-element.17.m_in, f32[128,128]{1,0:T(8,128)S(1)} %get-tuple-element.18.l_in, ...), custom_call_target="tpu_custom_call" | custom-call | tf_op jit(solution)/shard_map/exchange/pallas_call | solution.py:301
  41.9 6.1 %write.1 = (f32[128,31360]{1,0:T(8,128)}, f32[128,128]{1,0:T(8,128)}) custom-call(f32[128,30720]{1,0:T(8,128)S(1)} %get-tuple-element.14.z_ref, f32[128,640]{1,0:T(8,128)S(1)} %get-tuple-element.23.tail_ref, f32[128,128]{1,0:T(8,128)S(1)} %get-tuple-element.24.logz_ref, f32[128,128]{1,0:T(8,128)S(1)} %get-tuple-element.25.q_ref), custom_call_target="tpu_custom_call" | custom-call | tf_op jit(solution)/shard_map/write/pallas_call | solution.py:321

commit v5 on v4

--- a/solution.py
+++ b/solution.py
@@ -18,9 +18,9 @@
 
 def head_kernel(
     axis_name,
-    temp_ref, x_hbm, w_hbm, b_hbm, cand_hbm, emb_ref,
+    temp_hbm, x_hbm, w_hbm, b_hbm, cand_hbm, emb_ref,
     z_ref, e_tail, normed, m_ref, l_ref, q_ref, cand_hi, cand_lo, inv_ref,
-    ebuf, raw, zbuf, x_ref, w_ref, b_ref, cand_ref, e_sem, s_sem, tail_sem,
+    ebuf, raw, zbuf, x_ref, w_ref, b_ref, cand_ref, temp_ref, e_sem, s_sem, tail_sem,
 ):
     me = lax.axis_index(axis_name)
     rows, feat = x_hbm.shape
@@ -37,7 +37,8 @@
     tail = pltpu.make_async_copy(emb_ref.at[pl.ds(tiles * TILE, TILE)], e_tail, tail_sem)
     small = [
         pltpu.make_async_copy(src, dst, s_sem.at[i])
-        for i, (src, dst) in enumerate(((x_hbm, x_ref), (w_hbm, w_ref), (b_hbm, b_ref), (cand_hbm, cand_ref)))]
+        for i, (src, dst) in enumerate((
+            (x_hbm, x_ref), (w_hbm, w_ref), (b_hbm, b_ref), (cand_hbm, cand_ref), (temp_hbm, temp_ref)))]
     for c in small:
         c.start()
     for t in range(2):
@@ -281,7 +282,7 @@
                 pltpu.VMEM((MXU, feat), jnp.bfloat16), square, square, square, square_int, square_int,
                 pltpu.VMEM((8, LANES), f32),
             ),
-            in_specs=[pl.BlockSpec(memory_space=pltpu.SMEM)] + [pl.BlockSpec(memory_space=pl.ANY)] * 5,
+            in_specs=[pl.BlockSpec(memory_space=pl.ANY)] * 6,
             out_specs=(vmem,) * 9,
             scratch_shapes=[
                 pltpu.VMEM((DEPTH, TILE, feat), jnp.bfloat16),
@@ -291,8 +292,9 @@
                 pltpu.VMEM((feat,), jnp.bfloat16),
                 pltpu.VMEM((feat,), jnp.bfloat16),
                 pltpu.VMEM((rows, cands), jnp.int32),
+                pltpu.SMEM((1, 1), f32),
                 pltpu.SemaphoreType.DMA((DEPTH,)),
-                pltpu.SemaphoreType.DMA((4,)),
+                pltpu.SemaphoreType.DMA((5,)),
                 pltpu.SemaphoreType.DMA,
             ],
             compiler_params=pltpu.CompilerParams(vmem_limit_bytes=40 * 1024 * 1024),

time: 48.2 us -> 47.9 us (level)
  no operation moved by 1% of the time
where the time goes in v5:
time: 47.9 us; the launch traced here: 47.8 us
  Pallas kernels  46.5 us (97%)
  between operations  1.29 us (3%)
    pallas_call x1, Pallas kernels, per_device(): pl.pallas_call(functools.partial(head_kernel, axis_name), out_shape=(pltp...  29.4 us
    pallas_call x1, Pallas kernels, per_device(): pl.pallas_call(functools.partial(exchange_kernel, axis_name, n_dev, main...  11 us
    pallas_call x1, Pallas kernels, per_device(): pl.pallas_call(write_kernel, grid=(rows // 32,), out_shape=(jax.ShapeDtyp...  6.11 us

profile of v5, /device:TPU:0, one launch (start us, length us, event | category | flops | bytes accessed | tf_op | source)
XLA Modules:
  0.0 47.8 jit_solution(1040945255750414256)
XLA Ops:
  1.3 29.4 %head.1 = (f32[128,30720]{1,0:T(8,128)S(1)}, bf16[640,1536]{1,0:T(8,128)(2,1)S(1)}, bf16[256,1536]{1,0:T(8,128)(2,1)S(1)}, f32[128,128]{1,0:T(8,128)S(1)}, f32[1...) custom-call(f32[1,1]{1,0:T(1,128)} %bitcast.1.temp_hbm, ...), custom_call_target="tpu_custom_call" | custom-call | tf_op jit(solution)/shard_map/head/pallas_call | solution.py:278
  30.7 11.0 %exchange.1 = (f32[128,640]{1,0:T(8,128)S(1)}, f32[128,128]{1,0:T(8,128)S(1)}, f32[128,128]{1,0:T(8,128)S(1)}) custom-call(bf16[640,1536]{1,0:T(8,128)(2,1)S(1)} %get-tuple-element.15.e_ref, bf16[256,1536]{1,0:T(8,128)(2,1)S(1)} %get-tuple-element.16.normed, f32[128,128]{1,0:T(8,128)S(1)} %get-tuple-element.17.m_in, f32[128,128]{1,0:T(8,128)S(1)} %get-tuple-element.18.l_in, ...), custom_call_target="tpu_custom_call" | custom-call | tf_op jit(solution)/shard_map/exchange/pallas_call | solution.py:303
  41.7 6.1 %write.1 = (f32[128,31360]{1,0:T(8,128)}, f32[128,128]{1,0:T(8,128)}) custom-call(f32[128,30720]{1,0:T(8,128)S(1)} %get-tuple-element.14.z_ref, f32[128,640]{1,0:T(8,128)S(1)} %get-tuple-element.23.tail_ref, f32[128,128]{1,0:T(8,128)S(1)} %get-tuple-element.24.logz_ref, f32[128,128]{1,0:T(8,128)S(1)} %get-tuple-element.25.q_ref), custom_call_target="tpu_custom_call" | custom-call | tf_op jit(solution)/shard_map/write/pallas_call | solution.py:323

commit v6 on v5

--- a/solution.py
+++ b/solution.py
@@ -41,11 +41,11 @@
             (x_hbm, x_ref), (w_hbm, w_ref), (b_hbm, b_ref), (cand_hbm, cand_ref), (temp_hbm, temp_ref)))]
     for c in small:
         c.start()
-    for t in range(2):
+    for t in range(3):
         load(t, t).start()
     for c in small:
         c.wait()
-    for t in range(2, DEPTH - 1):
+    for t in range(3, DEPTH - 1):
         load(t, t).start()
 
     xf = x_ref[...].astype(jnp.float32)
@@ -226,9 +226,9 @@
     for k in range(1, n_dev):
         own = own + recv[k]
     q_own[...] = own
+    q_all[me] = own
     for c in ag_copies:
         c.start()
-    q_all[me] = own
     for c in stat_copies:
         c.wait_recv()
     tops = stat_recv[:, 0, :]

time: 47.9 us -> 47.9 us (level)
  no operation moved by 1% of the time
where the time goes in v6:
time: 47.9 us; the launch traced here: 47.8 us
  Pallas kernels  46.5 us (97%)
  between operations  1.29 us (3%)
    pallas_call x1, Pallas kernels, per_device(): pl.pallas_call(functools.partial(head_kernel, axis_name), out_shape=(pltp...  29.4 us
    pallas_call x1, Pallas kernels, per_device(): pl.pallas_call(functools.partial(exchange_kernel, axis_name, n_dev, main...  11 us
    pallas_call x1, Pallas kernels, per_device(): pl.pallas_call(write_kernel, grid=(rows // 32,), out_shape=(jax.ShapeDtyp...  6.11 us

profile of v6, /device:TPU:0, one launch (start us, length us, event | category | flops | bytes accessed | tf_op | source)
XLA Modules:
  0.0 47.8 jit_solution(515971673110838905)
XLA Ops:
  1.3 29.4 %head.1 = (f32[128,30720]{1,0:T(8,128)S(1)}, bf16[640,1536]{1,0:T(8,128)(2,1)S(1)}, bf16[256,1536]{1,0:T(8,128)(2,1)S(1)}, f32[128,128]{1,0:T(8,128)S(1)}, f32[1...) custom-call(f32[1,1]{1,0:T(1,128)} %bitcast.1.temp_hbm, ...), custom_call_target="tpu_custom_call" | custom-call | tf_op jit(solution)/shard_map/head/pallas_call | solution.py:278
  30.7 11.0 %exchange.1 = (f32[128,640]{1,0:T(8,128)S(1)}, f32[128,128]{1,0:T(8,128)S(1)}, f32[128,128]{1,0:T(8,128)S(1)}) custom-call(bf16[640,1536]{1,0:T(8,128)(2,1)S(1)} %get-tuple-element.15.e_ref, bf16[256,1536]{1,0:T(8,128)(2,1)S(1)} %get-tuple-element.16.normed, f32[128,128]{1,0:T(8,128)S(1)} %get-tuple-element.17.m_in, f32[128,128]{1,0:T(8,128)S(1)} %get-tuple-element.18.l_in, ...), custom_call_target="tpu_custom_call" | custom-call | tf_op jit(solution)/shard_map/exchange/pallas_call | solution.py:303
  41.7 6.1 %write.1 = (f32[128,31360]{1,0:T(8,128)}, f32[128,128]{1,0:T(8,128)}) custom-call(f32[128,30720]{1,0:T(8,128)S(1)} %get-tuple-element.14.z_ref, f32[128,640]{1,0:T(8,128)S(1)} %get-tuple-element.23.tail_ref, f32[128,128]{1,0:T(8,128)S(1)} %get-tuple-element.24.logz_ref, f32[128,128]{1,0:T(8,128)S(1)} %get-tuple-element.25.q_ref), custom_call_target="tpu_custom_call" | custom-call | tf_op jit(solution)/shard_map/write/pallas_call | solution.py:323

commit v7 on v6

--- a/solution.py
+++ b/solution.py
@@ -259,7 +259,10 @@
         for j in range(TILE // LANES):
             c = slice(j * LANES, (j + 1) * LANES)
             lp_ref[r, columns + j * LANES:columns + (j + 1) * LANES] = tail_ref[r, c] - norm
-    cand_lp_ref[...] = q_ref[...]
+
+    @pl.when(pl.program_id(0) == 0)
+    def _():
+        cand_lp_ref[...] = q_ref[...]
 
 
 def solution(mesh):
@@ -327,8 +330,9 @@
                 jax.ShapeDtypeStruct((rows, columns), f32),
                 jax.ShapeDtypeStruct((rows, cands), f32),
             ),
-            in_specs=[pl.BlockSpec((32, n), lambda i: (i, 0)) for n in (main, TILE, LANES, cands)],
-            out_specs=(pl.BlockSpec((32, columns), lambda i: (i, 0)), pl.BlockSpec((32, cands), lambda i: (i, 0))),
+            in_specs=[pl.BlockSpec((32, n), lambda i: (i, 0)) for n in (main, TILE, LANES)] + [
+                pl.BlockSpec((rows, cands), lambda i: (0, 0))],
+            out_specs=(pl.BlockSpec((32, columns), lambda i: (i, 0)), pl.BlockSpec((rows, cands), lambda i: (0, 0))),
             compiler_params=pltpu.CompilerParams(vmem_limit_bytes=24 * 1024 * 1024),
             name="write",
         )(z, z_tail, logz, q)

time: 47.9 us -> 47.9 us (level)
  no operation moved by 1% of the time
where the time goes in v7:
time: 47.9 us; the launch traced here: 47.8 us
  Pallas kernels  46.5 us (97%)
  between operations  1.29 us (3%)
    pallas_call x1, Pallas kernels, per_device(): pl.pallas_call(functools.partial(head_kernel, axis_name), out_shape=(pltp...  29.4 us
    pallas_call x1, Pallas kernels, per_device(): pl.pallas_call(functools.partial(exchange_kernel, axis_name, n_dev, main...  11 us
    pallas_call x1, Pallas kernels, per_device(): pl.pallas_call(write_kernel, grid=(rows // 32,), out_shape=(jax.ShapeDtyp...  6.09 us

profile of v7, /device:TPU:0, one launch (start us, length us, event | category | flops | bytes accessed | tf_op | source)
XLA Modules:
  0.0 47.8 jit_solution(7639269864838878856)
XLA Ops:
  1.3 29.4 %head.1 = (f32[128,30720]{1,0:T(8,128)S(1)}, bf16[640,1536]{1,0:T(8,128)(2,1)S(1)}, bf16[256,1536]{1,0:T(8,128)(2,1)S(1)}, f32[128,128]{1,0:T(8,128)S(1)}, f32[1...) custom-call(f32[1,1]{1,0:T(1,128)} %bitcast.1.temp_hbm, ...), custom_call_target="tpu_custom_call" | custom-call | tf_op jit(solution)/shard_map/head/pallas_call | solution.py:281
  30.7 11.0 %exchange.1 = (f32[128,640]{1,0:T(8,128)S(1)}, f32[128,128]{1,0:T(8,128)S(1)}, f32[128,128]{1,0:T(8,128)S(1)}) custom-call(bf16[640,1536]{1,0:T(8,128)(2,1)S(1)} %get-tuple-element.15.e_ref, bf16[256,1536]{1,0:T(8,128)(2,1)S(1)} %get-tuple-element.16.normed, f32[128,128]{1,0:T(8,128)S(1)} %get-tuple-element.17.m_in, f32[128,128]{1,0:T(8,128)S(1)} %get-tuple-element.18.l_in, ...), custom_call_target="tpu_custom_call" | custom-call | tf_op jit(solution)/shard_map/exchange/pallas_call | solution.py:306
  41.7 6.1 %write.1 = (f32[128,31360]{1,0:T(8,128)}, f32[128,128]{1,0:T(8,128)}) custom-call(f32[128,30720]{1,0:T(8,128)S(1)} %get-tuple-element.14.z_ref, f32[128,640]{1,0:T(8,128)S(1)} %get-tuple-element.23.tail_ref, f32[128,128]{1,0:T(8,128)S(1)} %get-tuple-element.24.logz_ref, f32[128,128]{1,0:T(8,128)S(1)} %get-tuple-element.25.q_ref), custom_call_target="tpu_custom_call" | custom-call | tf_op jit(solution)/shard_map/write/pallas_call | solution.py:326

commit v8 on v7

--- a/solution.py
+++ b/solution.py
@@ -41,11 +41,11 @@
             (x_hbm, x_ref), (w_hbm, w_ref), (b_hbm, b_ref), (cand_hbm, cand_ref), (temp_hbm, temp_ref)))]
     for c in small:
         c.start()
-    for t in range(3):
+    for t in range(4):
         load(t, t).start()
     for c in small:
         c.wait()
-    for t in range(3, DEPTH - 1):
+    for t in range(4, DEPTH - 1):
         load(t, t).start()
 
     xf = x_ref[...].astype(jnp.float32)

time: 47.9 us -> 47.9 us (level)
  no operation moved by 1% of the time
where the time goes in v8:
time: 47.9 us; the launch traced here: 47.8 us
  Pallas kernels  46.5 us (97%)
  between operations  1.29 us (3%)
    pallas_call x1, Pallas kernels, per_device(): pl.pallas_call(functools.partial(head_kernel, axis_name), out_shape=(pltp...  29.4 us
    pallas_call x1, Pallas kernels, per_device(): pl.pallas_call(functools.partial(exchange_kernel, axis_name, n_dev, main...  11 us
    pallas_call x1, Pallas kernels, per_device(): pl.pallas_call(write_kernel, grid=(rows // 32,), out_shape=(jax.ShapeDtyp...  6.09 us

profile of v8, /device:TPU:0, one launch (start us, length us, event | category | flops | bytes accessed | tf_op | source)
XLA Modules:
  0.0 47.8 jit_solution(11165389052627577776)
XLA Ops:
  1.3 29.4 %head.1 = (f32[128,30720]{1,0:T(8,128)S(1)}, bf16[640,1536]{1,0:T(8,128)(2,1)S(1)}, bf16[256,1536]{1,0:T(8,128)(2,1)S(1)}, f32[128,128]{1,0:T(8,128)S(1)}, f32[1...) custom-call(f32[1,1]{1,0:T(1,128)} %bitcast.1.temp_hbm, ...), custom_call_target="tpu_custom_call" | custom-call | tf_op jit(solution)/shard_map/head/pallas_call | solution.py:281
  30.7 11.0 %exchange.1 = (f32[128,640]{1,0:T(8,128)S(1)}, f32[128,128]{1,0:T(8,128)S(1)}, f32[128,128]{1,0:T(8,128)S(1)}) custom-call(bf16[640,1536]{1,0:T(8,128)(2,1)S(1)} %get-tuple-element.15.e_ref, bf16[256,1536]{1,0:T(8,128)(2,1)S(1)} %get-tuple-element.16.normed, f32[128,128]{1,0:T(8,128)S(1)} %get-tuple-element.17.m_in, f32[128,128]{1,0:T(8,128)S(1)} %get-tuple-element.18.l_in, ...), custom_call_target="tpu_custom_call" | custom-call | tf_op jit(solution)/shard_map/exchange/pallas_call | solution.py:306
  41.7 6.1 %write.1 = (f32[128,31360]{1,0:T(8,128)}, f32[128,128]{1,0:T(8,128)}) custom-call(f32[128,30720]{1,0:T(8,128)S(1)} %get-tuple-element.14.z_ref, f32[128,640]{1,0:T(8,128)S(1)} %get-tuple-element.23.tail_ref, f32[128,128]{1,0:T(8,128)S(1)} %get-tuple-element.24.logz_ref, f32[128,128]{1,0:T(8,128)S(1)} %get-tuple-element.25.q_ref), custom_call_target="tpu_custom_call" | custom-call | tf_op jit(solution)/shard_map/write/pallas_call | solution.py:326
